TPU v7x, 32 devices: a whole 2x2x4 slice. The times are simulated.
32 devices in a mesh: seq: 16 (over z, y, core), head: 2 (over x).
Axes of the slice: x: 2, y: 2, z: 4, core: 2. Of those that a mesh axis runs over, the one named last changes fastest.
Arguments:
- sequence: bfloat16 [8192, 2048], P('seq'), may hold values from -6 to 6
- input_weight: bfloat16 [2048, 4096], P(None, 'head'), may hold values from -0.125 to 0.125
- gate_weight: bfloat16 [2048, 4096], P(None, 'head'), may hold values from -0.125 to 0.125
- state_weight: bfloat16 [2048, 256], replicated, may hold values from -0.015625 to 0.015625
- step_weight: bfloat16 [2048, 64], P(None, 'head'), may hold values from -0.125 to 0.125
- step_bias: float32 [64], P('head'), may hold values from -2 to 0
- decay_rate: float32 [64], P('head'), may hold values from 6.1035156e-05 to 0.1
- skip_gain: float32 [64], P('head'), may hold values from 0.5 to 1.5
- output_weight: bfloat16 [4096, 2048], P('head'), may hold values from -0.09375 to 0.09375
Outputs:
- encoded: bfloat16 [8192, 2048], P('seq', 'head')
All inputs are finite; a program needn't handle non-finite values.
Results may differ from a plain program's by a relative error of at most 0.014.
Values sent between devices are 32-bit elements; how exact they have to be, the bound alone decides.
A program may use at most 128 MiB of HBM per device.

v0:
```python
import functools

import jax
import jax.numpy as jnp
from jax import lax
from jax.experimental import pallas as pl
from jax.experimental.pallas import tpu as pltpu
from jax.sharding import PartitionSpec as P

F32 = jnp.float32
BF16 = jnp.bfloat16
HEADDIM = 64
CHUNK = 128


def eye_flip(size):
    r = lax.broadcasted_iota(jnp.int32, (size, size), 0)
    c = lax.broadcasted_iota(jnp.int32, (size, size), 1)
    return jnp.where(r + c == size - 1, 1.0, 0.0).astype(BF16)


def flip_kernel(s_ref, o_ref):
    rows, width = s_ref.shape
    block = min(256, width)
    flip = eye_flip(block)
    count = width // block
    o_ref[:rows, :] = s_ref[...]
    for b in range(count):
        src = s_ref[:, (count - 1 - b) * block : (count - b) * block]
        o_ref[rows:, b * block : (b + 1) * block] = jnp.dot(
            src, flip, preferred_element_type=F32
        ).astype(BF16)


def stacked(sequence):
    rows, width = sequence.shape
    return pl.pallas_call(
        flip_kernel,
        out_shape=jax.ShapeDtypeStruct((2 * rows, width), BF16),
    )(sequence)


def pair_wide(cols, first):
    rows = cols.shape[0]
    lane = lax.broadcasted_iota(jnp.int32, (rows, 2 * HEADDIM), 1)
    return jnp.where(lane < HEADDIM, cols[:, first : first + 1], cols[:, first + 1 : first + 2])


def state_kernel(pairs, x_ref, b_ref, w_ref, o_ref):
    writer = b_ref[...]
    factor = w_ref[0]
    parts = []
    for p in range(pairs):
        x = x_ref[:, p * 128 : (p + 1) * 128].astype(F32)
        parts.append((x * pair_wide(factor, 2 * p)).astype(BF16))
    weighted = jnp.concatenate(parts, axis=1)
    o_ref[0] = lax.dot_general(
        writer, weighted, (((0,), (0,)), ((), ())), preferred_element_type=F32
    )


def local_states(inputs, state_proj, factor, rows):
    width = inputs.shape[1]
    state = state_proj.shape[1] // 2
    pairs = min(4, width // 128)
    groups = width // (128 * pairs)
    return pl.pallas_call(
        functools.partial(state_kernel, pairs),
        grid=(2, groups),
        in_specs=[
            pl.BlockSpec((rows, 128 * pairs), lambda d, g: (d, g)),
            pl.BlockSpec((rows, state), lambda d, g: (d, 0)),
            pl.BlockSpec((1, rows, 2 * pairs), lambda d, g: (d * groups + g, 0, 0)),
        ],
        out_specs=pl.BlockSpec((1, state, 128 * pairs), lambda d, g: (d, 0, g)),
        out_shape=jax.ShapeDtypeStruct((2, state, width), F32),
        compiler_params=pltpu.CompilerParams(dimension_semantics=("arbitrary", "arbitrary")),
    )(inputs, state_proj, factor)


def inside_kernel(pairs, state, x_ref, s_ref, ld_ref, ldt_ref, dt_ref, dtt_ref, skip_ref, o_ref, aff):
    branch = pl.program_id(0)
    rows = x_ref.shape[0]
    count = rows // CHUNK
    r = lax.broadcasted_iota(jnp.int32, (CHUNK, CHUNK), 0)
    c = lax.broadcasted_iota(jnp.int32, (CHUNK, CHUNK), 1)

    @pl.when(pl.program_id(1) == 0)
    def _():
        for k in range(count):
            at = slice(k * CHUNK, (k + 1) * CHUNK)
            aff[k] = lax.dot_general(
                s_ref[at, state:], s_ref[at, :state], (((1,), (1,)), ((), ())),
                preferred_element_type=F32,
            )

    lane = lax.broadcasted_iota(jnp.int32, (CHUNK, 128), 1)

    def run(ahead):
        keep = (r >= c) if ahead else (r <= c)
        ld = ld_ref[0]
        ldt = ldt_ref[0]
        dt = dt_ref[0]
        dtt = dtt_ref[0]
        order = range(count) if ahead else range(count - 1, -1, -1)
        carry = jnp.zeros((state, 128 * pairs), F32)
        edge_prev = None
        for step, k in enumerate(order):
            at = slice(k * CHUNK, (k + 1) * CHUNK)
            edge_row = (k + 1) * CHUNK - 1 if ahead else k * CHUNK
            ldk = ld[at, :]
            edge = ld[edge_row : edge_row + 1, :]
            since = jnp.exp(ldk) if step == 0 else jnp.exp(ldk - edge_prev)
            to_end = jnp.exp(edge - ldk) * dt[at, :]
            if step:
                carried = jnp.dot(s_ref[at, state:], carry.astype(BF16), preferred_element_type=F32)
            weighted = []
            for p in range(pairs):
                cols = slice(p * 128, (p + 1) * 128)
                x = x_ref[at, cols]
                xf = x.astype(F32)
                mixes = []
                for h in (2 * p, 2 * p + 1):
                    spread = jnp.where(keep, ldk[:, h : h + 1] - ldt[h : h + 1, at], 0.0)
                    mix = jnp.where(keep, aff[k] * jnp.exp(spread), 0.0) * dtt[h : h + 1, at]
                    mixes.append(mix.astype(BF16))
                zero = jnp.zeros_like(x)
                both = jnp.concatenate(
                    [jnp.where(lane < HEADDIM, x, zero), jnp.where(lane < HEADDIM, zero, x)], axis=0
                )
                out = jnp.dot(jnp.concatenate(mixes, axis=1), both, preferred_element_type=F32)
                out = out + xf * skip_ref[:, cols]
                if step:
                    out = out + carried[:, cols] * pair_wide(since, 2 * p)
                o_ref[at, cols] = out.astype(BF16)
                if step < count - 1:
                    weighted.append((xf * pair_wide(to_end, 2 * p)).astype(BF16))
            if step < count - 1:
                local = lax.dot_general(
                    s_ref[at, :state], jnp.concatenate(weighted, axis=1),
                    (((0,), (0,)), ((), ())), preferred_element_type=F32,
                )
                if step:
                    fade = jnp.exp(edge - edge_prev)
                    wide = jnp.concatenate([pair_wide(fade, 2 * p) for p in range(pairs)], axis=1)
                    carry = carry * wide + local
                else:
                    carry = local
            edge_prev = edge

    @pl.when(branch == 0)
    def _():
        run(True)

    @pl.when(branch == 1)
    def _():
        run(False)


def inside_of(inputs, state_proj, ld, ldt, dt, dtt, skip, rows):
    width = inputs.shape[1]
    state = state_proj.shape[1] // 2
    pairs = min(4, width // 128)
    groups = width // (128 * pairs)
    heads = 2 * pairs
    return pl.pallas_call(
        functools.partial(inside_kernel, pairs, state),
        grid=(2, groups),
        in_specs=[
            pl.BlockSpec((rows, 128 * pairs), lambda d, g: (d, g)),
            pl.BlockSpec((rows, 2 * state), lambda d, g: (d, 0)),
            pl.BlockSpec((1, rows, heads), lambda d, g: (d * groups + g, 0, 0)),
            pl.BlockSpec((1, heads, rows), lambda d, g: (d * groups + g, 0, 0)),
            pl.BlockSpec((1, rows, heads), lambda d, g: (d * groups + g, 0, 0)),
            pl.BlockSpec((1, heads, rows), lambda d, g: (d * groups + g, 0, 0)),
            pl.BlockSpec((1, 128 * pairs), lambda d, g: (0, g)),
        ],
        out_specs=pl.BlockSpec((rows, 128 * pairs), lambda d, g: (d, g)),
        out_shape=jax.ShapeDtypeStruct(inputs.shape, BF16),
        scratch_shapes=[pltpu.VMEM((rows // CHUNK, CHUNK, CHUNK), F32)],
        compiler_params=pltpu.CompilerParams(dimension_semantics=("arbitrary", "arbitrary")),
    )(inputs, state_proj, ld, ldt, dt, dtt, skip)


def gate_kernel(pairs, state, i_ref, g_ref, s_ref, ld_ref, c_ref, o_ref):
    reader = s_ref[:, state:]
    carried = jnp.dot(reader, c_ref[0].astype(BF16), preferred_element_type=F32)
    grown = jnp.exp(ld_ref[0])
    for p in range(pairs):
        cols = slice(p * 128, (p + 1) * 128)
        g = g_ref[:, cols].astype(F32)
        full = i_ref[:, cols].astype(F32) + carried[:, cols] * pair_wide(grown, 2 * p)
        o_ref[:, cols] = (full * (g / (1.0 + jnp.exp(-g)))).astype(BF16)


def gated_of(inside, gates, state_proj, ld, carry, rows):
    width = inside.shape[1]
    state = state_proj.shape[1] // 2
    pairs = min(4, width // 128)
    groups = width // (128 * pairs)
    heads = 2 * pairs
    tile = pl.BlockSpec((rows, 128 * pairs), lambda d, g: (d, g))
    return pl.pallas_call(
        functools.partial(gate_kernel, pairs, state),
        grid=(2, groups),
        in_specs=[
            tile,
            tile,
            pl.BlockSpec((rows, 2 * state), lambda d, g: (d, 0)),
            pl.BlockSpec((1, rows, heads), lambda d, g: (d * groups + g, 0, 0)),
            pl.BlockSpec((1, state, 128 * pairs), lambda d, g: (d, 0, g)),
        ],
        out_specs=tile,
        out_shape=jax.ShapeDtypeStruct(inside.shape, BF16),
        compiler_params=pltpu.CompilerParams(dimension_semantics=("arbitrary", "arbitrary")),
    )(inside, gates, state_proj, ld, carry)


def out_kernel(rows, at_ref, g_ref, w_ref, v_ref, o_ref):
    flipped = jnp.dot(v_ref[...], eye_flip(v_ref.shape[1]), preferred_element_type=F32).astype(BF16)
    acc = jnp.dot(g_ref[:rows, :], w_ref[...], preferred_element_type=F32)
    o_ref[...] = acc + jnp.dot(g_ref[rows:, :], flipped, preferred_element_type=F32)


def out_share(gated, weight, share, shares, rows):
    depth, columns = weight.shape
    wide = columns // shares
    block = min(256, wide)
    per = wide // block
    total = columns // block
    return pl.pallas_call(
        functools.partial(out_kernel, rows),
        grid_spec=pltpu.PrefetchScalarGridSpec(
            num_scalar_prefetch=1,
            grid=(per,),
            in_specs=[
                pl.BlockSpec(gated.shape, lambda j, at: (0, 0)),
                pl.BlockSpec((depth, block), lambda j, at: (0, at[0] * per + j)),
                pl.BlockSpec((depth, block), lambda j, at: (0, total - 1 - at[0] * per - j)),
            ],
            out_specs=pl.BlockSpec((rows, block), lambda j, at: (0, j)),
        ),
        out_shape=jax.ShapeDtypeStruct((rows, wide), F32),
        compiler_params=pltpu.CompilerParams(dimension_semantics=("arbitrary",)),
    )(share.reshape(1).astype(jnp.int32), gated, weight, weight)


def widen(logs):
    return jnp.repeat(jnp.exp(logs), HEADDIM, axis=-1)[..., None, :]


def entering(state, own, gate_of, inside_from, axis):
    n = lax.axis_size(axis)
    me = lax.axis_index(axis)
    top = min(n, 4)
    strides = []
    d = 1
    while n // d > top:
        strides.append(d)
        d *= 2

    saved = []
    tied = None if strides else gate_of(state)[1]
    for d in strides:
        if d == strides[-1]:
            state, tied = gate_of(state)
        half = state.shape[1] // 2
        upper = (me // d) % 2
        low, high = state[:, :half], state[:, half:]
        mine = jnp.where(upper == 0, low, high)
        other = jnp.where(upper == 0, high, low)
        got = lax.ppermute(other, axis, [(i, i ^ d) for i in range(n)])
        x = jnp.where(upper == 0, mine, got)
        y = jnp.where(upper == 0, got, mine)
        got_log = lax.ppermute(own, axis, [(i, i ^ d) for i in range(n)])
        ax = widen(jnp.where(upper == 0, own, got_log))
        ay = widen(jnp.where(upper == 0, got_log, own))
        own = own + got_log
        saved.append((d, upper, x, y, ax, ay))
        state = jnp.stack([ay[0] * x[0] + y[0], ax[1] * y[1] + x[1]])
    unit = n // top
    gates = tied
    state, gates = lax.optimization_barrier((state, gates))

    def shift(value, by):
        pairs = [(i, i + by * unit) for i in range(n) if 0 <= i + by * unit < n]
        return lax.ppermute(value, axis, pairs)

    before = jnp.stack([shift(own[0], 1), shift(own[1], -1)])
    own_w = widen(own)
    entry = [shift(state[0], 1), shift(state[1], -1)]
    if top > 2:
        summed = [own_w[k] * entry[k] + state[k] for k in (0, 1)]
        fade = widen(before)
        far = [shift(summed[0], 2), shift(summed[1], -2)]
        entry = [fade[k] * far[k] + entry[k] for k in (0, 1)]
    enter = jnp.stack(entry)
    enter, inside = inside_from(enter)
    first = True
    for d, upper, x, y, ax, ay in reversed(saved):
        low = jnp.stack([enter[0], ay[1] * enter[1] + y[1]])
        high = jnp.stack([ax[0] * enter[0] + x[0], enter[1]])
        mine = jnp.where(upper == 0, low, high)
        other = jnp.where(upper == 0, high, low)
        if not first:
            other, inside = lax.optimization_barrier((other, inside))
        first = False
        got = lax.ppermute(other, axis, [(i, i ^ d) for i in range(n)])
        enter = jnp.where(
            upper == 0,
            jnp.concatenate([mine, got], axis=1),
            jnp.concatenate([got, mine], axis=1),
        )
    return enter, gates, inside


def by_group(array, heads):
    two, rows, total = array.shape
    cols = array.reshape(two, rows, total // heads, heads)
    return (
        cols.transpose(0, 2, 1, 3).reshape(-1, rows, heads),
        cols.transpose(0, 2, 3, 1).reshape(-1, heads, rows),
    )


def on_device(
    sequence,
    input_weight,
    gate_weight,
    state_weight,
    step_weight,
    step_bias,
    decay_rate,
    skip_gain,
    output_weight,
):
    rows = sequence.shape[0]
    width = input_weight.shape[1]
    head_count = decay_rate.shape[0]
    group = 2 * min(4, width // 128)
    both = stacked(sequence)
    raw = jnp.dot(both, step_weight, preferred_element_type=F32) + step_bias[None, :]
    steps = jax.nn.softplus(raw).astype(BF16).astype(F32).reshape(2, rows, head_count)
    state_proj = jnp.dot(both, state_weight, preferred_element_type=F32).astype(BF16)
    r = lax.broadcasted_iota(jnp.int32, (rows, rows), 0)
    c = lax.broadcasted_iota(jnp.int32, (rows, rows), 1)
    tri = jnp.stack([(r >= c), (r <= c)]).astype(F32)
    ld = jnp.einsum(
        "bts,bsh->bth", tri, -decay_rate[None, None, :] * steps, precision=lax.Precision.HIGHEST
    )
    ends = jnp.stack([ld[0, -1], ld[1, 0]])
    factor = jnp.exp(ends[:, None, :] - ld) * steps
    ld_g, ldt_g = by_group(ld, group)
    dt_g, dtt_g = by_group(steps, group)
    factor_g, _ = by_group(factor, group)

    inputs = jnp.dot(both, input_weight, preferred_element_type=F32).astype(BF16)
    state = local_states(inputs, state_proj, factor_g, rows)
    skip = jnp.repeat(skip_gain, HEADDIM)[None, :]

    def gate_of(after):
        after, source = lax.optimization_barrier((after, both))
        return after, jnp.dot(source, gate_weight, preferred_element_type=F32).astype(BF16)

    def inside_from(after):
        after, source = lax.optimization_barrier((after, inputs))
        return after, inside_of(source, state_proj, ld_g, ldt_g, dt_g, dtt_g, skip, rows)

    carry, gates, inside = entering(state, ends, gate_of, inside_from, "seq")
    gated = gated_of(inside, gates, state_proj, ld_g, carry, rows)

    n = lax.axis_size("head")
    me = lax.axis_index("head")
    arrived = []
    cuts = 2
    for s in range(1, n):
        peer = lax.rem(me + s, n)
        pieces = []
        for k in range(cuts):
            part = out_share(gated, output_weight, cuts * peer + k, cuts * n, rows)
            pieces.append(lax.ppermute(part, "head", [(i, (i + s) % n) for i in range(n)]))
        arrived.append(jnp.concatenate(pieces, axis=1))
    total = out_share(gated, output_weight, me, n, rows)
    for part in arrived:
        total = total + part
    return total.astype(BF16)


def solution(mesh):
    placed = (
        P("seq", None),
        P(None, "head"),
        P(None, "head"),
        P(),
        P(None, "head"),
        P("head"),
        P("head"),
        P("head"),
        P("head", None),
    )
    return jax.shard_map(
        on_device, mesh=mesh, in_specs=placed, out_specs=P("seq", "head"), check_vma=False
    )
```

profile of v0, /device:TPU:0, one launch (start us, length us, event | category | flops | bytes accessed | tf_op | source)
XLA Modules:
  0.0 191.7 jit_solution(2157700845184284323)
XLA Ops:
  0.0 0.2 iota_compare_fusion
  0.2 4.3 %shard_map.91 = bf16[1024,2048]{1,0:T(8,128)(2,1)} custom-call(bf16[512,2048]{1,0:T(8,128)(2,1)} %s_ref.1), custom_call_target="tpu_custom_call" | custom-call | tf_op jit(solution)/shard_map/pallas_call | solution.py:37
  4.6 3.6 %fusion.7 = f32[1024,32]{0,1:T(8,128)S(1)} fusion(bf16[1024,2048]{1,0:T(8,128)(2,1)} %shard_map.91, bf16[2048,32]{0,1:T(8,128)(2,1)S(1)} %copy-done.10, f32[32]{0:T(128)S(1)} %copy-done.11), kind=kOutput, calls=%fused_computation.51 | convolution fusion | flops 134512640 | bytes 4456576 | tf_op jit(solution)/shard_map/dot_general | solution.py:342
  8.1 1.0 fusion.1
  9.2 0.2 slice_reduce_fusion.1
  9.4 0.6 collective-permute-start
  10.1 15.0 %convolution_convert_fusion.1.x_ref = bf16[1024,2048]{1,0:T(8,128)(2,1)} fusion(bf16[1024,2048]{1,0:T(8,128)(2,1)} %shard_map.91, bf16[2048,2048]{1,0:T(8,128)(2,1)} %param.10), kind=kOutput, calls=%fused_computation.1 | convolution fusion | flops 8592031744 | bytes 16777216 | tf_op jit(solution)/shard_map/dot_general | solution.py:357
  25.1 2.1 %convolution_convert_fusion.2.b_ref.s_ref = bf16[1024,256]{1,0:T(8,128)(2,1)} fusion(bf16[1024,2048]{1,0:T(8,128)(2,1)S(1)} %copy-done.2, bf16[2048,256]{1,0:T(8,128)(2,1)S(1)} %copy-done), kind=kOutput, calls=%fused_computation.7 | convolution fusion | flops 1074003968 | bytes 5767168 | tf_op jit(solution)/shard_map/dot_general | solution.py:344
  27.2 2.0 %copy.18 = f32[2,2048,8]{2,1,0:T(8,128)} copy(f32[2,2048,8]{1,2,0:T(8,128)S(1)} %pad_maximum_fusion.7) | data formatting | bytes 262144 | tf_op jit(solution)/shard_map/concatenate
  29.2 10.0 %shard_map.92 = f32[2,128,2048]{2,1,0:T(8,128)} custom-call(bf16[1024,2048]{1,0:T(8,128)(2,1)} %convolution_convert_fusion.1.x_ref, bf16[1024,256]{1,0:T(8,128)(2,1)} %convolution_convert_fusion.2.b_ref.s_ref, f32[8,512,8]{2,1,0:T(8,128)} %bitcast.76), custom_call_target="tpu_custom_call" | custom-call | tf_op jit(solution)/shard_map/pallas_call | solution.py:67
  39.2 1.8 slice_select_fusion
  41.1 3.0 %collective-permute-start.1 = (f32[2,32]{1,0:T(2,128)S(1)}, f32[2,32]{1,0:T(2,128)S(1)}, u32[]{:S(2)}, u32[]{:S(2)}) collective-permute-start(f32[2,32]{1,0:T(2,128)S(1)} %get-tuple-element.59), channel_id=1, source_target_pairs={{0,4},{2,6},{4,0},{6,2},{8,12},{10,14},{12,8},{14,10},{16,20},{18,... | collective-permute-start | bytes 776 | tf_op jit(solution)/shard_map/ppermute | solution.py:275
  44.4 1.3 collective-permute-done.1
  46.0 1.4 broadcast_select_fusion.1
  47.5 0.2 slice_add_fusion.1
  47.7 0.8 copy-done.5
  48.4 0.4 copy-done.7
  48.9 2.1 %collective-permute-start.5 = (f32[2,32,2048]{2,1,0:T(8,128)S(1)}, f32[2,32,2048]{2,1,0:T(8,128)S(1)}, u32[]{:S(2)}, u32[]{:S(2)}) collective-permute-start(f32[2,32,2048]{2,1,0:T(8,128)S(1)} %slice_select_fusion.2), channel_id=1, source_target_pairs={{0,4},{2,6},{4,0},{6,2},{8,12},{10,14},{12,8},{14,10},{16,20},{18,... | collective-permute-start | bytes 1572872 | tf_op jit(solution)/shard_map/ppermute | solution.py:272
  51.0 12.6 %convolution_convert_fusion.g_ref = bf16[1024,2048]{1,0:T(8,128)(2,1)} fusion(bf16[1024,2048]{1,0:T(8,128)(2,1)S(1)} %copy-done.3, bf16[2048,2048]{1,0:T(8,128)(2,1)} %param.11), kind=kOutput, calls=%fused_computation | convolution fusion | flops 8592031744 | bytes 16777216 | tf_op jit(solution)/shard_map/dot_general | solution.py:363
  63.9 1.3 collective-permute-start.8
  65.2 4.6 %collective-permute-start.6 = (f32[32,2048]{1,0:T(8,128)S(1)}, f32[32,2048]{1,0:T(8,128)S(1)}, u32[]{:S(2)}, u32[]{:S(2)}) collective-permute-start(f32[32,2048]{1,0:T(8,128)S(1)} %get-tuple-element.47), channel_id=1, source_target_pairs={{0,8},{2,10},{4,12},{6,14},{8,16},{10,18},{12,20},{14,22},{16,24},... | collective-permute-start | bytes 786440 | tf_op jit(solution)/shard_map/ppermute | solution.py:287
  70.1 1.3 collective-permute-start.3
  71.4 4.5 %collective-permute-start.2 = (f32[32]{0:T(128)S(1)}, f32[32]{0:T(128)S(1)}, u32[]{:S(2)}, u32[]{:S(2)}) collective-permute-start(f32[32]{0:T(128)S(1)} %get-tuple-element.72), channel_id=1, source_target_pairs={{0,8},{2,10},{4,12},{6,14},{8,16},{10,18},{12,20},{14,22},{16,24},... | collective-permute-start | bytes 392 | tf_op jit(solution)/shard_map/ppermute | solution.py:287
  76.3 1.3 collective-permute-start.9
  77.9 5.5 %collective-permute-start.7 = (f32[32,2048]{1,0:T(8,128)S(1)}, f32[32,2048]{1,0:T(8,128)S(1)}, u32[]{:S(2)}, u32[]{:S(2)}) collective-permute-start(f32[32,2048]{1,0:T(8,128)S(1)} %get-tuple-element.45), channel_id=1, source_target_pairs={{0,16},{2,18},{4,20},{6,22},{8,24},{10,26},{12,28},{14,30},{1,17},... | collective-permute-start | bytes 786440 | tf_op jit(solution)/shard_map/ppermute | solution.py:287
  83.4 7.0 %collective-permute-done.9 = f32[32,2048]{1,0:T(8,128)S(1)} collective-permute-done((f32[32,2048]{1,0:T(8,128)S(1)}, f32[32,2048]{1,0:T(8,128)S(1)}, u32[]{:S(2)}, u32[]{:S(2)}) %collective-permute-start.9) | collective-permute-done | bytes 262176 | tf_op jit(solution)/shard_map/ppermute | solution.py:287
  90.6 0.1 fusion.13
  90.7 0.1 fusion.5
  90.8 1.7 collective-permute-start.10
  92.6 1.9 copy.20
  94.5 0.7 copy.21
  95.2 1.9 copy.19
  97.1 0.7 broadcast_in_dim_reshape.2.skip_ref
  98.1 18.0 %shard_map.93.i_ref = bf16[1024,2048]{1,0:T(8,128)(2,1)} custom-call(bf16[1024,2048]{1,0:T(8,128)(2,1)} %convolution_convert_fusion.1.x_ref, bf16[1024,256]{1,0:T(8,128)(2,1)} %convolution_convert_fusion.2.b_ref.s_ref, f32[8,512,8]{2,1,0:T(8,128)} %bitcast.74, f32[8,8,512]{2,1,0:T(8,128)} %bitcast.82, f32[8,512,8]{2,1,0:T(8,128)} %bitcast.77, ...), custom_call_target="tpu_custom_call" | custom-call | tf_op jit(solution)/shard_map/pallas_call | solution.py:166
  116.1 1.4 maximum_select_fusion.1
  117.5 0.2 multiply_add_fusion.1
  117.8 0.2 fusion.2
  118.1 2.6 %collective-permute-done.11 = f32[2,64,2048]{2,1,0:T(8,128)S(1)} collective-permute-done((f32[2,64,2048]{2,1,0:T(8,128)S(1)}, f32[2,64,2048]{2,1,0:T(8,128)S(1)}, u32[]{:S(2)}, u32[]{:S(2)}) %collective-permute-start.11) | collective-permute-done | bytes 1048608 | tf_op jit(solution)/shard_map/ppermute | solution.py:308
  120.7 1.5 maximum_select_fusion.c_ref
  122.2 10.8 %shard_map.94.g_ref = bf16[1024,2048]{1,0:T(8,128)(2,1)} custom-call(bf16[1024,2048]{1,0:T(8,128)(2,1)} %shard_map.93.i_ref, bf16[1024,2048]{1,0:T(8,128)(2,1)} %convolution_convert_fusion.g_ref, bf16[1024,256]{1,0:T(8,128)(2,1)} %convolution_convert_fusion.2.b_ref.s_ref, f32[8,512,8]{2,1,0:T(8,128)} %bitcast.75, f32[2,128,2048]{2,1,0:T(8,128)} %maximum_select_fusion.c_ref), custom_call_target="tpu_custom_call" | custom-call | tf_op jit(solution)/shard_map/pallas_call | solution.py:203
  133.0 7.9 %shard_map.97 = f32[512,512]{1,0:T(8,128)} custom-call(s32[1]{0:T(128)} %bitcast.32.at_ref, bf16[1024,2048]{1,0:T(8,128)(2,1)} %shard_map.94.g_ref, bf16[2048,2048]{1,0:T(8,128)(2,1)} %v_ref.5, bf16[2048,2048]{1,0:T(8,128)(2,1)} %v_ref.5), custom_call_target="tpu_custom_call" | custom-call | tf_op jit(solution)/shard_map/pallas_call | solution.py:231
  140.9 1.5 collective-permute-start.13
  142.4 7.9 %shard_map.96 = f32[512,512]{1,0:T(8,128)} custom-call(s32[1]{0:T(128)} %bitcast.31.at_ref, bf16[1024,2048]{1,0:T(8,128)(2,1)} %shard_map.94.g_ref, bf16[2048,2048]{1,0:T(8,128)(2,1)} %v_ref.5, bf16[2048,2048]{1,0:T(8,128)(2,1)} %v_ref.5), custom_call_target="tpu_custom_call" | custom-call | tf_op jit(solution)/shard_map/pallas_call | solution.py:231
  150.4 0.5 collective-permute-start.12
  150.9 12.3 %shard_map.95 = f32[512,1024]{1,0:T(8,128)} custom-call(s32[1]{0:T(128)} %bitcast.at_ref, bf16[1024,2048]{1,0:T(8,128)(2,1)} %shard_map.94.g_ref, bf16[2048,2048]{1,0:T(8,128)(2,1)} %v_ref.5, bf16[2048,2048]{1,0:T(8,128)(2,1)} %v_ref.5), custom_call_target="tpu_custom_call" | custom-call | tf_op jit(solution)/shard_map/pallas_call | solution.py:231
  163.2 4.0 %collective-permute-done.13 = f32[512,512]{1,0:T(8,128)S(1)} collective-permute-done((f32[512,512]{1,0:T(8,128)}, f32[512,512]{1,0:T(8,128)S(1)}, u32[]{:S(2)}, u32[]{:S(2)}) %collective-permute-start.13) | collective-permute-done | bytes 1048608 | tf_op jit(solution)/shard_map/ppermute | solution.py:381
  167.2 21.6 %collective-permute-done.12 = f32[512,512]{1,0:T(8,128)S(1)} collective-permute-done((f32[512,512]{1,0:T(8,128)}, f32[512,512]{1,0:T(8,128)S(1)}, u32[]{:S(2)}, u32[]{:S(2)}) %collective-permute-start.12) | collective-permute-done | bytes 1048608 | tf_op jit(solution)/shard_map/ppermute | solution.py:381
  188.8 2.9 %fusion = bf16[512,1024]{1,0:T(8,128)(2,1)} fusion(f32[512,1024]{1,0:T(8,128)} %shard_map.95, f32[512,512]{1,0:T(8,128)S(1)} %collective-permute-done.13, f32[512,512]{1,0:T(8,128)S(1)} %collective-permute-done.12), kind=kLoop, calls=%fused_computation.4 | loop fusion | flops 1572864 | bytes 5242880 | tf_op jit(solution)/shard_map/convert_element_type | solution.py:386
  (89 shorter events, 2.8 us)
Async XLA Ops:
  0.0 25.1 %copy-start = (bf16[2048,256]{1,0:T(8,128)(2,1)S(1)}, bf16[2048,256]{1,0:T(8,128)(2,1)}, u32[]{:S(2)}) copy-start(bf16[2048,256]{1,0:T(8,128)(2,1)} %param.12) | copy-start | bytes 3145732
  0.0 4.5 %copy-start.13 = (f32[32]{0:T(128)S(1)}, f32[32]{0:T(128)}, u32[]{:S(2)}) copy-start(f32[32]{0:T(128)} %param.15) | copy-start | bytes 388
  0.0 4.5 %copy-start.10 = (bf16[2048,32]{0,1:T(8,128)(2,1)S(1)}, bf16[2048,32]{0,1:T(8,128)(2,1)}, u32[]{:S(2)}) copy-start(bf16[2048,32]{0,1:T(8,128)(2,1)} %param.13) | copy-start | bytes 393220
  0.0 4.5 %copy-start.11 = (f32[32]{0:T(128)S(1)}, f32[32]{0:T(128)}, u32[]{:S(2)}) copy-start(f32[32]{0:T(128)} %param.14) | copy-start | bytes 388
  9.2 86.0 %copy-start.9 = (f32[2,512,32]{1,2,0:T(8,128)}, f32[2,512,32]{1,2,0:T(8,128)S(1)}, u32[]{:S(2)}) copy-start(f32[2,512,32]{1,2,0:T(8,128)S(1)} %fusion.1) | copy-start | bytes 393220
  9.4 31.7 %collective-permute-start = (f32[2,32]{1,0:T(2,128)S(1)}, f32[2,32]{1,0:T(2,128)S(1)}, u32[]{:S(2)}, u32[]{:S(2)}) collective-permute-start(f32[2,32]{1,0:T(2,128)S(1)} %pad_maximum_fusion.9), channel_id=1, source_target_pairs={{0,2},{2,0},{4,6},{6,4},{8,10},{10,8},{12,14},{14,12},{16,18},{18,... | collective-permute-start | bytes 776 | tf_op jit(solution)/shard_map/ppermute | solution.py:275
  10.0 15.0 %copy-start.2 = (bf16[1024,2048]{1,0:T(8,128)(2,1)S(1)}, bf16[1024,2048]{1,0:T(8,128)(2,1)}, u32[]{:S(2)}) copy-start(bf16[1024,2048]{1,0:T(8,128)(2,1)} %shard_map.91) | copy-start | bytes 12582916
  39.1 6.9 %copy-start.4 = (f32[2,128,2048]{2,1,0:T(8,128)S(1)}, f32[2,128,2048]{2,1,0:T(8,128)}, u32[]{:S(2)}) copy-start(f32[2,128,2048]{2,1,0:T(8,128)} %shard_map.92) | copy-start | bytes 6291460
  41.0 5.0 %collective-permute-start.4 = (f32[2,64,2048]{2,1,0:T(8,128)S(1)}, f32[2,64,2048]{2,1,0:T(8,128)}, u32[]{:S(2)}, u32[]{:S(2)}) collective-permute-start(f32[2,64,2048]{2,1,0:T(8,128)S(1)} %slice_select_fusion), channel_id=1, source_target_pairs={{0,2},{2,0},{4,6},{6,4},{8,10},{10,8},{12,14},{14,12},{16,18},{18,... | collective-permute-start | bytes 3145736 | tf_op jit(solution)/shard_map/ppermute | solution.py:272
  41.1 4.6 %collective-permute-start.1 = (f32[2,32]{1,0:T(2,128)S(1)}, f32[2,32]{1,0:T(2,128)S(1)}, u32[]{:S(2)}, u32[]{:S(2)}) collective-permute-start(f32[2,32]{1,0:T(2,128)S(1)} %get-tuple-element.59), channel_id=1, source_target_pairs={{0,4},{2,6},{4,0},{6,2},{8,12},{10,14},{12,8},{14,10},{16,20},{18,... | collective-permute-start | bytes 776 | tf_op jit(solution)/shard_map/ppermute | solution.py:275
  47.5 1.0 copy-start.5
  47.5 1.3 copy-start.7
  47.5 3.5 %copy-start.3 = (bf16[1024,2048]{1,0:T(8,128)(2,1)S(1)}, bf16[1024,2048]{1,0:T(8,128)(2,1)}, u32[]{:S(2)}) copy-start(bf16[1024,2048]{1,0:T(8,128)(2,1)} %shard_map.91) | copy-start | bytes 12582916
  48.9 14.7 %collective-permute-start.5 = (f32[2,32,2048]{2,1,0:T(8,128)S(1)}, f32[2,32,2048]{2,1,0:T(8,128)S(1)}, u32[]{:S(2)}, u32[]{:S(2)}) collective-permute-start(f32[2,32,2048]{2,1,0:T(8,128)S(1)} %slice_select_fusion.2), channel_id=1, source_target_pairs={{0,4},{2,6},{4,0},{6,2},{8,12},{10,14},{12,8},{14,10},{16,20},{18,... | collective-permute-start | bytes 1572872 | tf_op jit(solution)/shard_map/ppermute | solution.py:272
  63.9 12.3 %collective-permute-start.8 = (f32[32,2048]{1,0:T(8,128)S(1)}, f32[32,2048]{1,0:T(8,128)S(1)}, u32[]{:S(2)}, u32[]{:S(2)}) collective-permute-start(f32[32,2048]{1,0:T(8,128)S(1)} %get-tuple-element.48), channel_id=1, source_target_pairs={{8,0},{10,2},{12,4},{14,6},{16,8},{18,10},{20,12},{22,14},{24,16},... | collective-permute-start | bytes 786440 | tf_op jit(solution)/shard_map/ppermute | solution.py:287
  65.2 11.0 %collective-permute-start.6 = (f32[32,2048]{1,0:T(8,128)S(1)}, f32[32,2048]{1,0:T(8,128)S(1)}, u32[]{:S(2)}, u32[]{:S(2)}) collective-permute-start(f32[32,2048]{1,0:T(8,128)S(1)} %get-tuple-element.47), channel_id=1, source_target_pairs={{0,8},{2,10},{4,12},{6,14},{8,16},{10,18},{12,20},{14,22},{16,24},... | collective-permute-start | bytes 786440 | tf_op jit(solution)/shard_map/ppermute | solution.py:287
  70.1 7.5 %collective-permute-start.3 = (f32[32]{0:T(128)S(1)}, f32[32]{0:T(128)S(1)}, u32[]{:S(2)}, u32[]{:S(2)}) collective-permute-start(f32[32]{0:T(128)S(1)} %get-tuple-element.73), channel_id=1, source_target_pairs={{8,0},{10,2},{12,4},{14,6},{16,8},{18,10},{20,12},{22,14},{24,16},... | collective-permute-start | bytes 392 | tf_op jit(solution)/shard_map/ppermute | solution.py:287
  71.4 6.2 %collective-permute-start.2 = (f32[32]{0:T(128)S(1)}, f32[32]{0:T(128)S(1)}, u32[]{:S(2)}, u32[]{:S(2)}) collective-permute-start(f32[32]{0:T(128)S(1)} %get-tuple-element.72), channel_id=1, source_target_pairs={{0,8},{2,10},{4,12},{6,14},{8,16},{10,18},{12,20},{14,22},{16,24},... | collective-permute-start | bytes 392 | tf_op jit(solution)/shard_map/ppermute | solution.py:287
  76.3 14.2 %collective-permute-start.9 = (f32[32,2048]{1,0:T(8,128)S(1)}, f32[32,2048]{1,0:T(8,128)S(1)}, u32[]{:S(2)}, u32[]{:S(2)}) collective-permute-start(f32[32,2048]{1,0:T(8,128)S(1)} %get-tuple-element.46), channel_id=1, source_target_pairs={{16,0},{18,2},{20,4},{22,6},{24,8},{26,10},{28,12},{30,14},{17,1},... | collective-permute-start | bytes 786440 | tf_op jit(solution)/shard_map/ppermute | solution.py:287
  77.9 12.6 %collective-permute-start.7 = (f32[32,2048]{1,0:T(8,128)S(1)}, f32[32,2048]{1,0:T(8,128)S(1)}, u32[]{:S(2)}, u32[]{:S(2)}) collective-permute-start(f32[32,2048]{1,0:T(8,128)S(1)} %get-tuple-element.45), channel_id=1, source_target_pairs={{0,16},{2,18},{4,20},{6,22},{8,24},{10,26},{12,28},{14,30},{1,17},... | collective-permute-start | bytes 786440 | tf_op jit(solution)/shard_map/ppermute | solution.py:287
  90.7 6.4 %copy-start.12 = (f32[32]{0:T(128)S(1)}, f32[32]{0:T(128)}, u32[]{:S(2)}) copy-start(f32[32]{0:T(128)} %param.16) | copy-start | bytes 388
  90.8 25.3 %collective-permute-start.10 = (f32[2,32,2048]{2,1,0:T(8,128)S(1)}, f32[2,32,2048]{2,1,0:T(8,128)}, u32[]{:S(2)}, u32[]{:S(2)}) collective-permute-start(f32[2,32,2048]{2,1,0:T(8,128)S(1)} %get-tuple-element.38), channel_id=1, source_target_pairs={{0,4},{2,6},{4,0},{6,2},{8,12},{10,14},{12,8},{14,10},{16,20},{18,... | collective-permute-start | bytes 1572872 | tf_op jit(solution)/shard_map/ppermute | solution.py:308
  98.1 19.4 %copy-start.6 = (f32[2,64,2048]{2,1,0:T(8,128)S(1)}, f32[2,64,2048]{2,1,0:T(8,128)}, u32[]{:S(2)}) copy-start(f32[2,64,2048]{2,1,0:T(8,128)} %copy-done.5) | copy-start | bytes 3145732
  98.1 19.4 %copy-start.8 = (f32[2,64,2048]{2,1,0:T(8,128)S(1)}, f32[2,64,2048]{2,1,0:T(8,128)}, u32[]{:S(2)}) copy-start(f32[2,64,2048]{2,1,0:T(8,128)} %copy-done.7) | copy-start | bytes 3145732
  118.0 2.7 %collective-permute-start.11 = (f32[2,64,2048]{2,1,0:T(8,128)S(1)}, f32[2,64,2048]{2,1,0:T(8,128)S(1)}, u32[]{:S(2)}, u32[]{:S(2)}) collective-permute-start(f32[2,64,2048]{2,1,0:T(8,128)S(1)} %get-tuple-element.20), channel_id=1, source_target_pairs={{0,2},{2,0},{4,6},{6,4},{8,10},{10,8},{12,14},{14,12},{16,18},{18,... | collective-permute-start | bytes 3145736 | tf_op jit(solution)/shard_map/ppermute | solution.py:308
  140.9 26.2 %collective-permute-start.13 = (f32[512,512]{1,0:T(8,128)}, f32[512,512]{1,0:T(8,128)S(1)}, u32[]{:S(2)}, u32[]{:S(2)}) collective-permute-start(f32[512,512]{1,0:T(8,128)} %shard_map.97), channel_id=1, source_target_pairs={{0,1},{1,0},{2,3},{3,2},{4,5},{5,4},{6,7},{7,6},{8,9},{9,8},{10,11... | collective-permute-start | bytes 3145736 | tf_op jit(solution)/shard_map/ppermute | solution.py:381
  150.4 38.5 %collective-permute-start.12 = (f32[512,512]{1,0:T(8,128)}, f32[512,512]{1,0:T(8,128)S(1)}, u32[]{:S(2)}, u32[]{:S(2)}) collective-permute-start(f32[512,512]{1,0:T(8,128)} %shard_map.96), channel_id=1, source_target_pairs={{0,1},{1,0},{2,3},{3,2},{4,5},{5,4},{6,7},{7,6},{8,9},{9,8},{10,11... | collective-permute-start | bytes 3145736 | tf_op jit(solution)/shard_map/ppermute | solution.py:381
  150.9 40.8 %copy-start.1 = (bf16[2048,256]{1,0:T(8,128)(2,1)S(1)}, bf16[2048,256]{1,0:T(8,128)(2,1)}, u32[]{:S(2)}) copy-start(bf16[2048,256]{1,0:T(8,128)(2,1)} %param.12) | copy-start | bytes 3145732
where the time goes:
time: 193 us; the launch traced here: 192 us
  Pallas kernels  71.2 us (37%)
  waiting for transfers between devices  36.6 us (19%)
  matrix products  34.3 us (18%)
  starting transfers between devices  28 us (15%)
  other arithmetic  10.6 us (5%)
  local copies, waits for them, and re-layouts  10.4 us (5%)
    pallas_call x3, Pallas kernels, out_share(): pl.pallas_call(functools.partial(out_kernel, rows), grid_spec=pltpu.Prefe...  28.1 us
    ppermute x2, waiting for transfers between devices, on_device(): lax.ppermute(part, 'head', [(i, (i + s) % n) for i in range(n)])  25.7 us
    ppermute x6, starting transfers between devices, shift(): return lax.ppermute(value, axis, pairs)  18.4 us
    pallas_call x1, Pallas kernels, inside_of(): pl.pallas_call(functools.partial(inside_kernel, pairs, state), grid=(2, g...  18 us
    dot_general x1, matrix products, on_device(): jnp.dot(both, input_weight, preferred_element_type=F32).astype(BF16)  15 us
    dot_general x1, matrix products, gate_of(): jnp.dot(source, gate_weight, preferred_element_type=F32).astype(BF16)  12.6 us
    pallas_call x1, Pallas kernels, gated_of(): pl.pallas_call(functools.partial(gate_kernel, pairs, state), grid=(2, gro...  10.8 us
    pallas_call x1, Pallas kernels, local_states(): pl.pallas_call(functools.partial(state_kernel, pairs), grid=(2, groups),...  9.96 us
  transfers between devices with their start and end apart: 14, of which 5 were waited for; matrix products, arithmetic and copies ran while one was open for 21% of the time, Pallas kernels for 25%

commit v1 on v0

v1 whole, which is shorter than its diff:
```python
import functools

import jax
import jax.numpy as jnp
from jax import lax
from jax.experimental import pallas as pl
from jax.experimental.pallas import tpu as pltpu
from jax.sharding import PartitionSpec as P

F32 = jnp.float32
BF16 = jnp.bfloat16
HEADDIM = 64
CHUNK = 128
LANES = 128
BLOCK = 256
STEP = 8


def eye_flip(size):
    r = lax.broadcasted_iota(jnp.int32, (size, size), 0)
    c = lax.broadcasted_iota(jnp.int32, (size, size), 1)
    return jnp.where(r + c == size - 1, 1.0, 0.0).astype(BF16)


def dot(a, b):
    return jnp.dot(a, b, preferred_element_type=F32)


def dot_first(a, b):
    return lax.dot_general(a, b, (((0,), (0,)), ((), ())), preferred_element_type=F32)


def dot_last(a, b):
    return lax.dot_general(a, b, (((1,), (1,)), ((), ())), preferred_element_type=F32)


def split(a):
    hi = a.astype(BF16)
    rest = a - hi.astype(F32)
    mid = rest.astype(BF16)
    low = (rest - mid.astype(F32)).astype(BF16)
    return hi, mid, low


def split_lanes(a, heads):
    hi, mid, low = split(a)
    lane = lax.broadcasted_iota(jnp.int32, a.shape, 1)
    low = jnp.where(lane < 3 * heads, low.astype(F32), 0.0)
    return jnp.where(
        lane < heads, hi.astype(F32), jnp.where(lane < 2 * heads, mid.astype(F32), low)
    ).astype(BF16)


def repeat_of(heads):
    r = lax.broadcasted_iota(jnp.int32, (heads, LANES), 0)
    c = lax.broadcasted_iota(jnp.int32, (heads, LANES), 1)
    hit = (c == r) | (c == r + heads) | (c == r + 2 * heads)
    return jnp.where(hit, 1.0, 0.0).astype(BF16)


def spread_of(heads, first, cols):
    r = lax.broadcasted_iota(jnp.int32, (LANES, cols), 0)
    c = lax.broadcasted_iota(jnp.int32, (LANES, cols), 1)
    head = lax.shift_right_logical(c, 6) + first
    hit = (r == head) | (r == head + heads) | (r == head + 2 * heads)
    return jnp.where(hit, 1.0, 0.0).astype(BF16)


def layer_kernel(
    plan,
    x_ref, stw_ref, sw_ref, bias_ref, rate_ref, gain_ref, inw_ref, gw_ref, ow_ref,
    out_ref,
    xf, proj, ldg, ldt, dtt, fac3, sin3, end3, spread, aff, skipw, logs, coef,
    wbuf, obuf, inp, gates, gated,
    ups, gots, chin, chout, ents, outs, sbuf, rbuf,
    w_sem, o_sem, lg_send, lg_recv, up_send, up_recv, ch_send, ch_recv, dn_send, dn_recv,
    x_send, x_recv,
):
    (groups, cols, levels, top, unit, n, peers, heads, per, total) = plan
    rows, depth = x_ref.shape
    state = stw_ref.shape[1] // 2
    hg = cols // HEADDIM
    tiles = cols // LANES
    count = rows // CHUNK
    me = lax.axis_index("seq")
    side = lax.axis_index("head")
    pos = me // unit
    bits = [(me // (1 << l)) % 2 for l in range(levels)]

    def mate(j):
        at = me
        for l in range(levels):
            if (j >> l) & 1:
                at = at + (1 << l) * (1 - 2 * bits[l])
        return at

    def ring(step):
        return me + (lax.rem(pos + step + top, top) - pos) * unit

    def w_copy(src, g):
        return pltpu.make_async_copy(
            src.at[:, pl.ds(pl.multiple_of(g * cols, LANES), cols)], wbuf.at[g], w_sem.at[g]
        )

    def o_copy(b):
        return pltpu.make_async_copy(
            ow_ref.at[:, pl.ds(b * BLOCK, BLOCK)], obuf.at[b], o_sem.at[b]
        )

    for g in range(groups):
        w_copy(inw_ref, g).start()

    barrier = pltpu.get_barrier_semaphore()
    greet = [mate(j) for j in range(1, 1 << levels)] + [ring(1), ring(-1)]
    for who in greet:
        pl.semaphore_signal(barrier, inc=1, device_id={"seq": who})
    for s in range(1, peers):
        pl.semaphore_signal(barrier, inc=1, device_id={"head": lax.rem(side + s, peers)})
    for d in (0, 1):
        @pl.when((pos if d == 0 else top - 1 - pos) == 0)
        def _():
            chin[:, d] = jnp.zeros_like(chin[:, d])
    pl.semaphore_wait(barrier, len(greet) + peers - 1)

    flip = eye_flip(BLOCK)
    blocks = depth // BLOCK
    for b in range(blocks):
        xf[:, b * BLOCK : (b + 1) * BLOCK] = dot(
            x_ref[:, (blocks - 1 - b) * BLOCK : (blocks - b) * BLOCK], flip
        ).astype(BF16)
    rep = repeat_of(heads)
    for g in range(groups):
        spread[g] = spread_of(heads, g * hg, cols)
    sw3 = dot(sw_ref[...], rep).astype(BF16)

    def tripled(ref):
        wide = jnp.broadcast_to(ref[...], (8, heads))
        a, b, c = split(wide)
        return dot(a, rep) + dot(b, rep) + dot(c, rep)

    bias = tripled(bias_ref)[0:1]
    rate = tripled(rate_ref)[0:1]
    gain = split_lanes(tripled(gain_ref), heads)
    for g in range(groups):
        skipw[g] = dot(gain, spread[g])
    r = lax.broadcasted_iota(jnp.int32, (rows, rows), 0)
    c = lax.broadcasted_iota(jnp.int32, (rows, rows), 1)
    for d in (0, 1):
        src = x_ref if d == 0 else xf
        raw = dot(src[...], sw3) + bias
        soft = jnp.maximum(raw, 0.0) + jnp.log1p(jnp.exp(-jnp.abs(raw)))
        steps = soft.astype(BF16).astype(F32)
        proj[d] = dot(src[...], stw_ref[...]).astype(BF16)
        tri = jnp.where((r >= c) if d == 0 else (r <= c), 1.0, 0.0).astype(BF16)
        va, vb, vc = split(-rate * steps)
        ld = dot(tri, va) + dot(tri, vb) + dot(tri, vc)
        end = ld[rows - 1 : rows] if d == 0 else ld[0:1]
        fac3[d] = split_lanes(jnp.exp(end - ld) * steps, heads)
        for k in range(count):
            at = slice(k * CHUNK, (k + 1) * CHUNK)
            ldk = ld[at]
            if d == 0:
                edge = ld[(k + 1) * CHUNK - 1 : (k + 1) * CHUNK]
                prev = ld[k * CHUNK - 1 : k * CHUNK] if k else None
            else:
                edge = ld[k * CHUNK : k * CHUNK + 1]
                prev = ld[(k + 1) * CHUNK : (k + 1) * CHUNK + 1] if k < count - 1 else None
            sin3[d, at] = split_lanes(jnp.exp(ldk if prev is None else ldk - prev), heads)
            end3[d, at] = split_lanes(jnp.exp(edge - ldk) * steps[at], heads)
            aff[d, k] = dot_last(proj[d, at, state:], proj[d, at, :state])
        flat_ld = ld.T
        flat_dt = steps.T
        ends = split_lanes(jnp.broadcast_to(end, (8, LANES)), heads)
        for g in range(groups):
            ldg[d, g] = pltpu.roll(ld, LANES - g * hg, axis=1) if g else ld
            ldt[d, g] = flat_ld[g * hg : (g + 1) * hg]
            dtt[d, g] = flat_dt[g * hg : (g + 1) * hg]
            wide = dot(ends, spread[g])
            for j in range(tiles):
                logs[0, d, g, j : j + 1] = wide[0:1, j * LANES : (j + 1) * LANES]

    def log_copy(j):
        return pltpu.make_async_remote_copy(
            src_ref=logs.at[0], dst_ref=logs.at[j], send_sem=lg_send.at[j],
            recv_sem=lg_recv.at[j], device_id={"seq": mate(j)},
        )

    def half_of(l):
        return state >> (l + 1)

    def rows_at(l, flag):
        return pl.ds(pl.multiple_of(flag * half_of(l), 8), half_of(l))

    def up_copy(l, g):
        return pltpu.make_async_remote_copy(
            src_ref=ups[l].at[g, :, rows_at(l, 1 - bits[l]), :], dst_ref=gots[l].at[g],
            send_sem=up_send.at[l, g], recv_sem=up_recv.at[l, g],
            device_id={"seq": mate(1 << l)},
        )

    def chain_copy(d, g):
        return pltpu.make_async_remote_copy(
            src_ref=chout.at[g, d], dst_ref=chin.at[g, d], send_sem=ch_send.at[d, g],
            recv_sem=ch_recv.at[d, g], device_id={"seq": ring(1 if d == 0 else -1)},
        )

    def down_copy(l, g):
        return pltpu.make_async_remote_copy(
            src_ref=outs[l].at[g], dst_ref=ents[l].at[g, :, rows_at(l, bits[l]), :],
            send_sem=dn_send.at[l, g], recv_sem=dn_recv.at[l, g],
            device_id={"seq": mate(1 << l)},
        )

    def late(l, d):
        flag = bits[l] if d == 0 else 1 - bits[l]
        return flag.astype(F32)

    def own_coef(l, d, g):
        return coef[2 * l, d, g]

    def other_coef(l, d, g):
        return coef[2 * l + 1, d, g]

    def combine(l, g):
        mine = rows_at(l, bits[l])
        for d in (0, 1):
            f = late(l, d)
            ea = f + (1.0 - f) * other_coef(l, d, g)
            eb = (1.0 - f) + f * own_coef(l, d, g)
            for j in range(tiles):
                at = slice(j * LANES, (j + 1) * LANES)
                ups[l + 1][g, d, :, at] = (
                    ea[j : j + 1] * ups[l][g, d, mine, at] + eb[j : j + 1] * gots[l][g, d, :, at]
                )

    def scatter_down(l, g):
        mine = rows_at(l, bits[l])
        for d in (0, 1):
            f = late(l, d)
            keep = f * other_coef(l, d, g) + (1.0 - f)
            give = f + (1.0 - f) * own_coef(l, d, g)
            for j in range(tiles):
                at = slice(j * LANES, (j + 1) * LANES)
                enter = chin[g, d, :, at] if l == levels - 1 else ents[l + 1][g, d, :, at]
                outs[l][g, d, :, at] = (
                    give[j : j + 1] * enter + (1.0 - f) * ups[l][g, d, mine, at]
                )
                ents[l][g, d, mine, at] = keep[j : j + 1] * enter + f * gots[l][g, d, :, at]

    def order(d):
        return pos if d == 0 else top - 1 - pos

    def hop(h, g, ok):
        for d in (0, 1):
            @pl.when(ok & (order(d) == h))
            def _():
                if h:
                    chain_copy(d, g).wait_recv()
                whole = coef[2 * levels, d, g]
                for j in range(tiles):
                    at = slice(j * LANES, (j + 1) * LANES)
                    chout[g, d, :, at] = (
                        whole[j : j + 1] * chin[g, d, :, at] + ups[levels][g, d, :, at]
                    )
                chain_copy(d, g).start()

    for j in range(1, 1 << levels):
        log_copy(j).start()

    def states(g):
        w_copy(inw_ref, g).wait()
        for d in (0, 1):
            src = x_ref if d == 0 else xf
            x = dot(src[...], wbuf[g]).astype(BF16)
            inp[g, d] = x
            wide = dot(fac3[d], spread[g])
            weighted = (inp[g, d].astype(F32) * wide).astype(BF16)
            ups[0][g, d] = dot_first(proj[d, :, :state], weighted)

    def gate(g):
        w_copy(gw_ref, g).wait()
        for d in (0, 1):
            src = x_ref if d == 0 else xf
            gates[g, d] = dot(src[...], wbuf[g]).astype(BF16)

    tr = lax.broadcasted_iota(jnp.int32, (CHUNK, CHUNK), 0)
    tc = lax.broadcasted_iota(jnp.int32, (CHUNK, CHUNK), 1)
    lane = lax.broadcasted_iota(jnp.int32, (CHUNK, LANES), 1)

    def finish(g):
        for d in (0, 1):
            keep = (tr >= tc) if d == 0 else (tr <= tc)
            carry = ents[0][g, d]
            skip = skipw[g][0:1]
            for step in range(count):
                k = step if d == 0 else count - 1 - step
                at = slice(k * CHUNK, (k + 1) * CHUNK)
                ldk = ldg[d, g, at, :]
                since = dot(sin3[d, at], spread[g])
                last = step == count - 1
                carried = dot(proj[d, at, state:], carry.astype(BF16)) * since
                weighted = []
                if not last:
                    to_end = dot(end3[d, at], spread[g])
                for p in range(tiles):
                    part = slice(p * LANES, (p + 1) * LANES)
                    x = inp[g, d, at, part]
                    xf32 = x.astype(F32)
                    mixes = []
                    for h in (2 * p, 2 * p + 1):
                        gap = ldk[:, h : h + 1] - ldt[d, g, h : h + 1, at]
                        gap = jnp.where(keep, gap, 0.0)
                        mix = jnp.where(keep, aff[d, k] * jnp.exp(gap), 0.0)
                        mixes.append((mix * dtt[d, g, h : h + 1, at]).astype(BF16))
                    zero = jnp.zeros_like(x)
                    both = jnp.concatenate(
                        [jnp.where(lane < HEADDIM, x, zero), jnp.where(lane < HEADDIM, zero, x)],
                        axis=0,
                    )
                    out = dot(jnp.concatenate(mixes, axis=1), both)
                    out = out + xf32 * skip[:, part] + carried[:, part]
                    gt = gates[g, d, at, part].astype(F32)
                    out = (out * (gt / (1.0 + jnp.exp(-gt)))).astype(BF16)
                    where = pl.ds(pl.multiple_of(g * cols + p * LANES, LANES), LANES)
                    gated[d, at, where] = out
                    if not last:
                        weighted.append((xf32 * to_end[:, part]).astype(BF16))
                if not last:
                    local = dot_first(proj[d, at, :state], jnp.concatenate(weighted, axis=1))
                    row = CHUNK - 1 if d == 0 else 0
                    carry = carry * since[row : row + 1] + local

    lag = 2 * levels + top - 1
    start = max(2 * groups, lag + 1)

    def slot(s, _):
        @pl.when(s < groups)
        def _():
            states(s)
            up_copy(0, s).start()
            w_copy(gw_ref, s).start()

        @pl.when((s >= groups) & (s < 2 * groups))
        def _():
            gate(s - groups)

        @pl.when(s >= start)
        def _():
            finish(s - start)

        @pl.when(s == 0)
        def _():
            for b in range(total):
                o_copy(b).start()
            for j in range(1, 1 << levels):
                log_copy(j).wait()
            own = logs[0]
            for l in range(levels):
                other = logs[1 << l]
                for j in range((1 << l) + 1, 2 << l):
                    other = other + logs[j]
                coef[2 * l] = jnp.exp(own)
                coef[2 * l + 1] = jnp.exp(other)
                own = own + other
            coef[2 * levels] = jnp.exp(own)

        def stage(off, body):
            g = s - off
            ok = (g >= 0) & (g < groups)

            @pl.when(ok)
            def _():
                body(g)

        for l in range(levels):
            def up(g, l=l):
                up_copy(l, g).wait()
                combine(l, g)
                if l + 1 < levels:
                    up_copy(l + 1, g).start()

            stage(1 + l, up)
        for h in range(top - 1):
            g = s - (levels + h)
            hop(h, g, (g >= 0) & (g < groups))

        def arrive(g):
            for d in (0, 1):
                @pl.when(order(d) == top - 1)
                def _():
                    chain_copy(d, g).wait_recv()

                @pl.when(order(d) < top - 1)
                def _():
                    chain_copy(d, g).wait_send()
            scatter_down(levels - 1, g)
            down_copy(levels - 1, g).start()

        stage(levels + top - 1, arrive)
        for l in range(levels - 1, -1, -1):
            def down(g, l=l):
                down_copy(l, g).wait()
                if l:
                    scatter_down(l - 1, g)
                    down_copy(l - 1, g).start()

            stage(levels + top - 1 + levels - l, down)
        return 0

    lax.fori_loop(0, start + groups, slot, 0)

    for b in range(total):
        o_copy(b).wait()

    def share(b):
        turned = dot(obuf[total - 1 - b], flip).astype(BF16)
        return dot(gated[0], obuf[b]) + dot(gated[1], turned)

    def x_copy(i):
        s = i // per
        return pltpu.make_async_remote_copy(
            src_ref=sbuf.at[i], dst_ref=rbuf.at[i], send_sem=x_send.at[i], recv_sem=x_recv.at[i],
            device_id={"head": lax.rem(side + 1 + s, peers)},
        )

    def give(i, _):
        peer = lax.rem(side + 1 + i // per, peers)
        sbuf[i] = share(peer * per + i % per)
        x_copy(i).start()
        return 0

    lax.fori_loop(0, (peers - 1) * per, give, 0)
    for j in range(per):
        sbuf_own = share(side * per + j)
        for s in range(peers - 1):
            x_copy(s * per + j).wait()
            sbuf_own = sbuf_own + rbuf[s * per + j]
        out_ref[:, j * BLOCK : (j + 1) * BLOCK] = sbuf_own.astype(BF16)


def on_device(
    sequence, input_weight, gate_weight, state_weight, step_weight, step_bias, decay_rate,
    skip_gain, output_weight,
):
    rows, depth = sequence.shape
    width = input_weight.shape[1]
    heads = decay_rate.shape[0]
    state = state_weight.shape[1] // 2
    n = lax.axis_size("seq")
    peers = lax.axis_size("head")
    top = min(n, 4)
    unit = n // top
    levels = unit.bit_length() - 1
    cols = max(LANES, width // 4)
    groups = width // cols
    columns = output_weight.shape[1]
    per = columns // peers // BLOCK
    total = columns // BLOCK
    hg = cols // HEADDIM
    count = rows // CHUNK
    plan = (groups, cols, levels, top, unit, n, peers, heads, per, total)
    moves = (peers - 1) * per
    vmem = pl.BlockSpec(memory_space=pltpu.VMEM)
    hbm = pl.BlockSpec(memory_space=pl.ANY)
    dma = pltpu.SemaphoreType.DMA
    ups = [pltpu.VMEM((groups, 2, state >> l, cols), F32) for l in range(levels + 1)]
    halves = [pltpu.VMEM((groups, 2, state >> (l + 1), cols), F32) for l in range(levels)]
    ents = [pltpu.VMEM((groups, 2, state >> l, cols), F32) for l in range(levels)]
    chain = pltpu.VMEM((groups, 2, state >> levels, cols), F32)
    return pl.pallas_call(
        functools.partial(layer_kernel, plan),
        in_specs=[vmem] * 6 + [hbm] * 3,
        out_specs=vmem,
        out_shape=jax.ShapeDtypeStruct((rows, columns // peers), BF16),
        scratch_shapes=[
            pltpu.VMEM((rows, depth), BF16),
            pltpu.VMEM((2, rows, 2 * state), BF16),
            pltpu.VMEM((2, groups, rows, LANES), F32),
            pltpu.VMEM((2, groups, hg, rows), F32),
            pltpu.VMEM((2, groups, hg, rows), F32),
            pltpu.VMEM((2, rows, LANES), BF16),
            pltpu.VMEM((2, rows, LANES), BF16),
            pltpu.VMEM((2, rows, LANES), BF16),
            pltpu.VMEM((groups, LANES, cols), BF16),
            pltpu.VMEM((2, count, CHUNK, CHUNK), F32),
            pltpu.VMEM((groups, 8, cols), F32),
            pltpu.VMEM((1 << levels, 2, groups, STEP, LANES), F32),
            pltpu.VMEM((2 * levels + 1, 2, groups, STEP, LANES), F32),
            pltpu.VMEM((groups, depth, cols), BF16),
            pltpu.VMEM((total, width, BLOCK), BF16),
            pltpu.VMEM((groups, 2, rows, cols), BF16),
            pltpu.VMEM((groups, 2, rows, cols), BF16),
            pltpu.VMEM((2, rows, width), BF16),
            ups,
            halves,
            chain,
            chain,
            ents,
            halves,
            pltpu.VMEM((moves, rows, BLOCK), F32),
            pltpu.VMEM((moves, rows, BLOCK), F32),
            dma((groups,)),
            dma((total,)),
            dma((1 << levels,)),
            dma((1 << levels,)),
            dma((levels, groups)),
            dma((levels, groups)),
            dma((2, groups)),
            dma((2, groups)),
            dma((levels, groups)),
            dma((levels, groups)),
            dma((moves,)),
            dma((moves,)),
        ],
        compiler_params=pltpu.CompilerParams(
            collective_id=0, has_side_effects=True, vmem_limit_bytes=66_000_000
        ),
    )(
        sequence, state_weight, step_weight, step_bias.reshape(1, heads),
        decay_rate.reshape(1, heads), skip_gain.reshape(1, heads), input_weight, gate_weight,
        output_weight,
    )


def solution(mesh):
    placed = (
        P("seq", None),
        P(None, "head"),
        P(None, "head"),
        P(),
        P(None, "head"),
        P("head"),
        P("head"),
        P("head"),
        P("head", None),
    )
    return jax.shard_map(
        on_device, mesh=mesh, in_specs=placed, out_specs=P("seq", "head"), check_vma=False
    )
```

time: 193 us -> 112 us (0.58)
  waiting for transfers between devices: 36.6 us -> 0 us
  Pallas kernels: 71.2 us -> 107 us
  matrix products: 34.3 us -> 0 us
  starting transfers between devices: 28 us -> 0 us
  other arithmetic: 10.6 us -> 0 us
  local copies, waits for them, and re-layouts: 10.4 us -> 4.17 us
    ppermute x14 -> x0, waiting for transfers between devices: 36.6 us -> none  [the longest x2 25.7 us: on_device(): lax.ppermute(part, 'head', [(i, (i + s) % n) for i in range(n)])]
    pallas_call x7 -> x1, Pallas kernels: 71.2 us -> 107 us  [on_device(): pl.pallas_call(functools.partial(layer_kernel, plan), in_specs=[vmem] * 6...]
    dot_general x5 -> x0, matrix products: 34.3 us -> none  [the longest x1 15 us: on_device(): jnp.dot(both, input_weight, preferred_element_type=F32).astype(BF16)]
    ppermute x14 -> x0, starting transfers between devices: 28 us -> none  [the longest x6 18.4 us: shift(): return lax.ppermute(value, axis, pairs)]
    select_n x8 -> x0, other arithmetic: 6.6 us -> none  [the longest x2 2.89 us: entering(): jnp.where(upper == 0, jnp.concatenate([mine, got], axis=1), jnp.concatena...]
    another operation x6 -> x0, local copies, waits for them, and re-layouts: 5.16 us -> none  [the longest x2 2.56 us: by_group(): cols = array.reshape(two, rows, total // heads, heads)]
    unnamed x28 -> x2, local copies, waits for them, and re-layouts: 1.21 us -> 4.17 us
    convert_element_type x1 -> x0, other arithmetic: 2.85 us -> none  [on_device(): return total.astype(BF16)]
  transfers between devices with their start and end apart: 14 -> 0, of which waited for: 5 -> 0; matrix products, arithmetic and copies ran while one was open for 21% -> 0% of each run, Pallas kernels for 25% -> 0%
where the time goes in v1:
time: 112 us
  Pallas kernels  107 us (96%)
  local copies, waits for them, and re-layouts  4.17 us (4%)
    pallas_call x1, Pallas kernels, on_device(): pl.pallas_call(functools.partial(layer_kernel, plan), in_specs=[vmem] * 6...  107 us
    unnamed x2, local copies, waits for them, and re-layouts  4.17 us

profile of v1, /device:TPU:0, one launch (start us, length us, event | category | flops | bytes accessed | tf_op | source)
XLA Modules:
  0.0 111.6 jit_solution(10644972265685363644)
XLA Ops:
  0.0 1.9 %copy.10.sw_ref = bf16[2048,32]{1,0:T(8,128)(2,1)} copy(bf16[2048,32]{0,1:T(8,128)(2,1)} %param.13) | data formatting | bytes 262144 | tf_op args[4]
  1.9 107.5 %shard_map.91 = bf16[512,1024]{1,0:T(8,128)(2,1)} custom-call(bf16[512,2048]{1,0:T(8,128)(2,1)} %x_ref.1, bf16[2048,256]{1,0:T(8,128)(2,1)} %stw_ref.1, bf16[2048,32]{1,0:T(8,128)(2,1)} %copy.10.sw_ref, f32[1,32]{1,0:T(1,128)} %bitcast.3, f32[1,32]{1,0:T(1,128)} %bitcast.4, f32[1,32]{1,0:T(1,128)} %bitcast.5, bf16[2048,2048]{1,0:T(8,128)(2,1)} %inw_ref.1, ...), custom_call_target="tpu_custom_call" | custom-call | tf_op jit(solution)/shard_map/pallas_call | solution.py:470
  109.4 2.3 %copy.12 = bf16[512,1024]{1,0:T(8,128)(2,1)} copy(bf16[512,1024]{1,0:T(8,128)(2,1)} %shard_map.91) | data formatting | bytes 2097152

commit v2 on v1

--- a/solution.py
+++ b/solution.py
@@ -13,7 +13,9 @@
 CHUNK = 128
 LANES = 128
 BLOCK = 256
-STEP = 8
+GROUPS = 4
+FAR = 3
+HOP = 2
 
 
 def eye_flip(size):
@@ -24,10 +26,6 @@
 
 def dot(a, b):
     return jnp.dot(a, b, preferred_element_type=F32)
-
-
-def dot_first(a, b):
-    return lax.dot_general(a, b, (((0,), (0,)), ((), ())), preferred_element_type=F32)
 
 
 def dot_last(a, b):
@@ -51,9 +49,10 @@
     ).astype(BF16)
 
 
-def repeat_of(heads):
-    r = lax.broadcasted_iota(jnp.int32, (heads, LANES), 0)
-    c = lax.broadcasted_iota(jnp.int32, (heads, LANES), 1)
+def repeat_of(heads, turned=False):
+    shape = (LANES, heads) if turned else (heads, LANES)
+    r = lax.broadcasted_iota(jnp.int32, shape, 1 if turned else 0)
+    c = lax.broadcasted_iota(jnp.int32, shape, 0 if turned else 1)
     hit = (c == r) | (c == r + heads) | (c == r + 2 * heads)
     return jnp.where(hit, 1.0, 0.0).astype(BF16)
 
@@ -68,12 +67,12 @@
 
 def layer_kernel(
     plan,
-    x_ref, stw_ref, sw_ref, bias_ref, rate_ref, gain_ref, inw_ref, gw_ref, ow_ref,
+    sw_ref, bias_ref, rate_ref, gain_ref, x_hbm, stw_hbm, inw_ref, gw_ref, ow_ref,
     out_ref,
-    xf, proj, ldg, ldt, dtt, fac3, sin3, end3, spread, aff, skipw, logs, coef,
+    x_ref, stw_ref, xf, ldv, stv, proj, turned_b, ldg, ldt, dtt, fac3, sin3, end3, spread, aff, skipw, logs, coef,
     wbuf, obuf, inp, gates, gated,
     ups, gots, chin, chout, ents, outs, sbuf, rbuf,
-    w_sem, o_sem, lg_send, lg_recv, up_send, up_recv, ch_send, ch_recv, dn_send, dn_recv,
+    in_sem, w_sem, o_sem, lg_send, lg_recv, up_send, up_recv, ch_send, ch_recv, dn_send, dn_recv,
     x_send, x_recv,
 ):
     (groups, cols, levels, top, unit, n, peers, heads, per, total) = plan
@@ -107,6 +106,10 @@
             ow_ref.at[:, pl.ds(b * BLOCK, BLOCK)], obuf.at[b], o_sem.at[b]
         )
 
+    x_in = pltpu.make_async_copy(x_hbm, x_ref, in_sem.at[0])
+    stw_in = pltpu.make_async_copy(stw_hbm, stw_ref, in_sem.at[1])
+    x_in.start()
+    stw_in.start()
     for g in range(groups):
         w_copy(inw_ref, g).start()
 
@@ -120,42 +123,56 @@
         @pl.when((pos if d == 0 else top - 1 - pos) == 0)
         def _():
             chin[:, d] = jnp.zeros_like(chin[:, d])
-    pl.semaphore_wait(barrier, len(greet) + peers - 1)
-
+    rep = repeat_of(heads)
+    sw3 = dot(repeat_of(heads, True), sw_ref[...]).astype(BF16)
+
+    def tripled(ref):
+        wide = jnp.broadcast_to(ref[...], (8, heads))
+        a, b, c = split(wide)
+        return dot(a, rep) + dot(b, rep) + dot(c, rep)
+
+    bias = tripled(bias_ref)[0:1]
+    rate = tripled(rate_ref)[0:1]
+    for g in range(groups):
+        spread[g] = spread_of(heads, g * hg, cols)
     flip = eye_flip(BLOCK)
     blocks = depth // BLOCK
+    x_in.wait()
     for b in range(blocks):
         xf[:, b * BLOCK : (b + 1) * BLOCK] = dot(
             x_ref[:, (blocks - 1 - b) * BLOCK : (blocks - b) * BLOCK], flip
         ).astype(BF16)
-    rep = repeat_of(heads)
-    for g in range(groups):
-        spread[g] = spread_of(heads, g * hg, cols)
-    sw3 = dot(sw_ref[...], rep).astype(BF16)
-
-    def tripled(ref):
-        wide = jnp.broadcast_to(ref[...], (8, heads))
-        a, b, c = split(wide)
-        return dot(a, rep) + dot(b, rep) + dot(c, rep)
-
-    bias = tripled(bias_ref)[0:1]
-    rate = tripled(rate_ref)[0:1]
-    gain = split_lanes(tripled(gain_ref), heads)
-    for g in range(groups):
-        skipw[g] = dot(gain, spread[g])
     r = lax.broadcasted_iota(jnp.int32, (rows, rows), 0)
     c = lax.broadcasted_iota(jnp.int32, (rows, rows), 1)
     for d in (0, 1):
         src = x_ref if d == 0 else xf
-        raw = dot(src[...], sw3) + bias
+        raw = dot_last(src[...], sw3) + bias
         soft = jnp.maximum(raw, 0.0) + jnp.log1p(jnp.exp(-jnp.abs(raw)))
         steps = soft.astype(BF16).astype(F32)
-        proj[d] = dot(src[...], stw_ref[...]).astype(BF16)
         tri = jnp.where((r >= c) if d == 0 else (r <= c), 1.0, 0.0).astype(BF16)
         va, vb, vc = split(-rate * steps)
         ld = dot(tri, va) + dot(tri, vb) + dot(tri, vc)
         end = ld[rows - 1 : rows] if d == 0 else ld[0:1]
         fac3[d] = split_lanes(jnp.exp(end - ld) * steps, heads)
+        ldv[d] = ld
+        stv[d] = steps
+        ends = split_lanes(jnp.broadcast_to(end, (8, LANES)), heads)
+        for g in range(groups):
+            wide = dot(ends, spread[g])
+            for j in range(tiles):
+                row = g * tiles + j
+                logs[0, d, row : row + 1] = wide[0:1, j * LANES : (j + 1) * LANES]
+    stw_in.wait()
+    for d in (0, 1):
+        src = x_ref if d == 0 else xf
+        both = dot(src[...], stw_ref[...])
+        proj[d] = both.astype(BF16)
+        turned_b[d] = both[:, :state].T.astype(BF16)
+    pl.semaphore_wait(barrier, len(greet) + peers - 1)
+
+    def tables(d):
+        ld = ldv[d]
+        steps = stv[d]
         for k in range(count):
             at = slice(k * CHUNK, (k + 1) * CHUNK)
             ldk = ld[at]
@@ -167,17 +184,18 @@
                 prev = ld[(k + 1) * CHUNK : (k + 1) * CHUNK + 1] if k < count - 1 else None
             sin3[d, at] = split_lanes(jnp.exp(ldk if prev is None else ldk - prev), heads)
             end3[d, at] = split_lanes(jnp.exp(edge - ldk) * steps[at], heads)
-            aff[d, k] = dot_last(proj[d, at, state:], proj[d, at, :state])
+            aff[d, k] = dot(proj[d, at, state:], turned_b[d, :, at])
         flat_ld = ld.T
         flat_dt = steps.T
-        ends = split_lanes(jnp.broadcast_to(end, (8, LANES)), heads)
         for g in range(groups):
             ldg[d, g] = pltpu.roll(ld, LANES - g * hg, axis=1) if g else ld
             ldt[d, g] = flat_ld[g * hg : (g + 1) * hg]
             dtt[d, g] = flat_dt[g * hg : (g + 1) * hg]
-            wide = dot(ends, spread[g])
-            for j in range(tiles):
-                logs[0, d, g, j : j + 1] = wide[0:1, j * LANES : (j + 1) * LANES]
+
+    def skips():
+        gain = split_lanes(tripled(gain_ref), heads)
+        for g in range(groups):
+            skipw[g] = dot(gain, spread[g])
 
     def log_copy(j):
         return pltpu.make_async_remote_copy(
@@ -215,141 +233,147 @@
         flag = bits[l] if d == 0 else 1 - bits[l]
         return flag.astype(F32)
 
-    def own_coef(l, d, g):
-        return coef[2 * l, d, g]
-
-    def other_coef(l, d, g):
-        return coef[2 * l + 1, d, g]
+    def own_coef(l, d, g, j):
+        return coef[2 * l, d, pl.ds(g * tiles + j, 1), :]
+
+    def other_coef(l, d, g, j):
+        return coef[2 * l + 1, d, pl.ds(g * tiles + j, 1), :]
 
     def combine(l, g):
         mine = rows_at(l, bits[l])
         for d in (0, 1):
             f = late(l, d)
-            ea = f + (1.0 - f) * other_coef(l, d, g)
-            eb = (1.0 - f) + f * own_coef(l, d, g)
             for j in range(tiles):
+                ea = f + (1.0 - f) * other_coef(l, d, g, j)
+                eb = (1.0 - f) + f * own_coef(l, d, g, j)
                 at = slice(j * LANES, (j + 1) * LANES)
                 ups[l + 1][g, d, :, at] = (
-                    ea[j : j + 1] * ups[l][g, d, mine, at] + eb[j : j + 1] * gots[l][g, d, :, at]
+                    ea * ups[l][g, d, mine, at] + eb * gots[l][g, d, :, at]
                 )
 
     def scatter_down(l, g):
         mine = rows_at(l, bits[l])
         for d in (0, 1):
             f = late(l, d)
-            keep = f * other_coef(l, d, g) + (1.0 - f)
-            give = f + (1.0 - f) * own_coef(l, d, g)
             for j in range(tiles):
+                keep = f * other_coef(l, d, g, j) + (1.0 - f)
+                give = f + (1.0 - f) * own_coef(l, d, g, j)
                 at = slice(j * LANES, (j + 1) * LANES)
                 enter = chin[g, d, :, at] if l == levels - 1 else ents[l + 1][g, d, :, at]
                 outs[l][g, d, :, at] = (
-                    give[j : j + 1] * enter + (1.0 - f) * ups[l][g, d, mine, at]
+                    give * enter + (1.0 - f) * ups[l][g, d, mine, at]
                 )
-                ents[l][g, d, mine, at] = keep[j : j + 1] * enter + f * gots[l][g, d, :, at]
+                ents[l][g, d, mine, at] = keep * enter + f * gots[l][g, d, :, at]
 
     def order(d):
         return pos if d == 0 else top - 1 - pos
 
-    def hop(h, g, ok):
+    def hop(h, g):
         for d in (0, 1):
-            @pl.when(ok & (order(d) == h))
+            @pl.when(order(d) == h)
             def _():
                 if h:
                     chain_copy(d, g).wait_recv()
-                whole = coef[2 * levels, d, g]
                 for j in range(tiles):
                     at = slice(j * LANES, (j + 1) * LANES)
+                    whole = coef[2 * levels, d, pl.ds(g * tiles + j, 1), :]
                     chout[g, d, :, at] = (
-                        whole[j : j + 1] * chin[g, d, :, at] + ups[levels][g, d, :, at]
+                        whole * chin[g, d, :, at] + ups[levels][g, d, :, at]
                     )
                 chain_copy(d, g).start()
 
     for j in range(1, 1 << levels):
         log_copy(j).start()
 
-    def states(g):
-        w_copy(inw_ref, g).wait()
-        for d in (0, 1):
-            src = x_ref if d == 0 else xf
-            x = dot(src[...], wbuf[g]).astype(BF16)
-            inp[g, d] = x
-            wide = dot(fac3[d], spread[g])
-            weighted = (inp[g, d].astype(F32) * wide).astype(BF16)
-            ups[0][g, d] = dot_first(proj[d, :, :state], weighted)
-
-    def gate(g):
-        w_copy(gw_ref, g).wait()
-        for d in (0, 1):
-            src = x_ref if d == 0 else xf
-            gates[g, d] = dot(src[...], wbuf[g]).astype(BF16)
+    def states(g, d):
+        if d == 0:
+            w_copy(inw_ref, g).wait()
+        src = x_ref if d == 0 else xf
+        x = dot(src[...], wbuf[g]).astype(BF16)
+        inp[g, d] = x
+        wide = dot(fac3[d], spread[g])
+        weighted = (inp[g, d].astype(F32) * wide).astype(BF16)
+        ups[0][g, d] = dot(turned_b[d], weighted)
+
+    def gate(g, d):
+        if d == 0:
+            w_copy(gw_ref, g).wait()
+        src = x_ref if d == 0 else xf
+        gates[g, d] = dot(src[...], wbuf[g]).astype(BF16)
 
     tr = lax.broadcasted_iota(jnp.int32, (CHUNK, CHUNK), 0)
     tc = lax.broadcasted_iota(jnp.int32, (CHUNK, CHUNK), 1)
     lane = lax.broadcasted_iota(jnp.int32, (CHUNK, LANES), 1)
 
-    def finish(g):
-        for d in (0, 1):
-            keep = (tr >= tc) if d == 0 else (tr <= tc)
-            carry = ents[0][g, d]
-            skip = skipw[g][0:1]
-            for step in range(count):
-                k = step if d == 0 else count - 1 - step
-                at = slice(k * CHUNK, (k + 1) * CHUNK)
-                ldk = ldg[d, g, at, :]
-                since = dot(sin3[d, at], spread[g])
-                last = step == count - 1
-                carried = dot(proj[d, at, state:], carry.astype(BF16)) * since
-                weighted = []
+    def finish(g, d):
+        keep = (tr >= tc) if d == 0 else (tr <= tc)
+        carry = ents[0][g, d]
+        skip = skipw[g][0:1]
+        for step in range(count):
+            k = step if d == 0 else count - 1 - step
+            at = slice(k * CHUNK, (k + 1) * CHUNK)
+            ldk = ldg[d, g, at, :]
+            since = dot(sin3[d, at], spread[g])
+            last = step == count - 1
+            carried = dot(proj[d, at, state:], carry.astype(BF16)) * since
+            weighted = []
+            if not last:
+                to_end = dot(end3[d, at], spread[g])
+            for p in range(tiles):
+                part = slice(p * LANES, (p + 1) * LANES)
+                x = inp[g, d, at, part]
+                xf32 = x.astype(F32)
+                mixes = []
+                for h in (2 * p, 2 * p + 1):
+                    gap = ldk[:, h : h + 1] - ldt[d, g, h : h + 1, at]
+                    gap = jnp.where(keep, gap, 0.0)
+                    mix = jnp.where(keep, aff[d, k] * jnp.exp(gap), 0.0)
+                    mixes.append((mix * dtt[d, g, h : h + 1, at]).astype(BF16))
+                zero = jnp.zeros_like(x)
+                both = jnp.concatenate(
+                    [jnp.where(lane < HEADDIM, x, zero), jnp.where(lane < HEADDIM, zero, x)],
+                    axis=0,
+                )
+                out = dot(jnp.concatenate(mixes, axis=1), both)
+                out = out + xf32 * skip[:, part] + carried[:, part]
+                gt = gates[g, d, at, part].astype(F32)
+                out = (out * (gt / (1.0 + jnp.exp(-gt)))).astype(BF16)
+                where = pl.ds(pl.multiple_of(g * cols + p * LANES, LANES), LANES)
+                gated[d, at, where] = out
                 if not last:
-                    to_end = dot(end3[d, at], spread[g])
-                for p in range(tiles):
-                    part = slice(p * LANES, (p + 1) * LANES)
-                    x = inp[g, d, at, part]
-                    xf32 = x.astype(F32)
-                    mixes = []
-                    for h in (2 * p, 2 * p + 1):
-                        gap = ldk[:, h : h + 1] - ldt[d, g, h : h + 1, at]
-                        gap = jnp.where(keep, gap, 0.0)
-                        mix = jnp.where(keep, aff[d, k] * jnp.exp(gap), 0.0)
-                        mixes.append((mix * dtt[d, g, h : h + 1, at]).astype(BF16))
-                    zero = jnp.zeros_like(x)
-                    both = jnp.concatenate(
-                        [jnp.where(lane < HEADDIM, x, zero), jnp.where(lane < HEADDIM, zero, x)],
-                        axis=0,
-                    )
-                    out = dot(jnp.concatenate(mixes, axis=1), both)
-                    out = out + xf32 * skip[:, part] + carried[:, part]
-                    gt = gates[g, d, at, part].astype(F32)
-                    out = (out * (gt / (1.0 + jnp.exp(-gt)))).astype(BF16)
-                    where = pl.ds(pl.multiple_of(g * cols + p * LANES, LANES), LANES)
-                    gated[d, at, where] = out
-                    if not last:
-                        weighted.append((xf32 * to_end[:, part]).astype(BF16))
-                if not last:
-                    local = dot_first(proj[d, at, :state], jnp.concatenate(weighted, axis=1))
-                    row = CHUNK - 1 if d == 0 else 0
-                    carry = carry * since[row : row + 1] + local
-
-    lag = 2 * levels + top - 1
-    start = max(2 * groups, lag + 1)
-
-    def slot(s, _):
-        @pl.when(s < groups)
-        def _():
-            states(s)
-            up_copy(0, s).start()
-            w_copy(gw_ref, s).start()
-
-        @pl.when((s >= groups) & (s < 2 * groups))
-        def _():
-            gate(s - groups)
-
-        @pl.when(s >= start)
-        def _():
-            finish(s - start)
-
-        @pl.when(s == 0)
-        def _():
+                    weighted.append((xf32 * to_end[:, part]).astype(BF16))
+            if not last:
+                local = dot(turned_b[d, :, at], jnp.concatenate(weighted, axis=1))
+                row = CHUNK - 1 if d == 0 else 0
+                carry = carry * since[row : row + 1] + local
+
+    lat = [1] + [FAR] * (levels - 1)
+    up_at = [sum(lat[: l + 1]) for l in range(levels)]
+    hop_at = [up_at[-1] + HOP * h for h in range(top)]
+    down_at = [hop_at[-1] + sum(lat[l:]) for l in range(levels)]
+    lag = down_at[0]
+    start = max(groups + 1, lag // 2 + 1)
+
+    def half_slot(i, half):
+        def during(first, body, length=groups):
+            @pl.when((i >= first) & (i < first + length))
+            def _():
+                body(i - first)
+
+        def open_group(g):
+            states(g, half)
+            if half:
+                up_copy(0, g).start()
+                w_copy(gw_ref, g).start()
+
+        during(0, open_group)
+        during(groups, lambda g: gate(g, half))
+        during(groups, lambda _: tables(half), 1)
+        if half:
+            during(groups + 1, lambda _: skips(), 1)
+        during(start, lambda g: finish(g, half))
+
+        def first(_):
             for b in range(total):
                 o_copy(b).start()
             for j in range(1, 1 << levels):
@@ -364,13 +388,12 @@
                 own = own + other
             coef[2 * levels] = jnp.exp(own)
 
+        if half == 0:
+            during(1, first, 1)
+
         def stage(off, body):
-            g = s - off
-            ok = (g >= 0) & (g < groups)
-
-            @pl.when(ok)
-            def _():
-                body(g)
+            if (1 + off - half) % 2 == 0:
+                during((1 + off - half) // 2, body)
 
         for l in range(levels):
             def up(g, l=l):
@@ -379,10 +402,9 @@
                 if l + 1 < levels:
                     up_copy(l + 1, g).start()
 
-            stage(1 + l, up)
+            stage(up_at[l], up)
         for h in range(top - 1):
-            g = s - (levels + h)
-            hop(h, g, (g >= 0) & (g < groups))
+            stage(hop_at[h], lambda g, h=h: hop(h, g))
 
         def arrive(g):
             for d in (0, 1):
@@ -396,7 +418,7 @@
             scatter_down(levels - 1, g)
             down_copy(levels - 1, g).start()
 
-        stage(levels + top - 1, arrive)
+        stage(hop_at[-1], arrive)
         for l in range(levels - 1, -1, -1):
             def down(g, l=l):
                 down_copy(l, g).wait()
@@ -404,7 +426,11 @@
                     scatter_down(l - 1, g)
                     down_copy(l - 1, g).start()
 
-            stage(levels + top - 1 + levels - l, down)
+            stage(down_at[l], down)
+
+    def slot(i, _):
+        half_slot(i, 0)
+        half_slot(i, 1)
         return 0
 
     lax.fori_loop(0, start + groups, slot, 0)
@@ -451,7 +477,7 @@
     top = min(n, 4)
     unit = n // top
     levels = unit.bit_length() - 1
-    cols = max(LANES, width // 4)
+    cols = max(LANES, width // GROUPS)
     groups = width // cols
     columns = output_weight.shape[1]
     per = columns // peers // BLOCK
@@ -469,12 +495,17 @@
     chain = pltpu.VMEM((groups, 2, state >> levels, cols), F32)
     return pl.pallas_call(
         functools.partial(layer_kernel, plan),
-        in_specs=[vmem] * 6 + [hbm] * 3,
+        in_specs=[vmem] * 4 + [hbm] * 5,
         out_specs=vmem,
         out_shape=jax.ShapeDtypeStruct((rows, columns // peers), BF16),
         scratch_shapes=[
             pltpu.VMEM((rows, depth), BF16),
+            pltpu.VMEM((depth, 2 * state), BF16),
+            pltpu.VMEM((rows, depth), BF16),
+            pltpu.VMEM((2, rows, LANES), F32),
+            pltpu.VMEM((2, rows, LANES), F32),
             pltpu.VMEM((2, rows, 2 * state), BF16),
+            pltpu.VMEM((2, state, rows), BF16),
             pltpu.VMEM((2, groups, rows, LANES), F32),
             pltpu.VMEM((2, groups, hg, rows), F32),
             pltpu.VMEM((2, groups, hg, rows), F32),
@@ -484,8 +515,8 @@
             pltpu.VMEM((groups, LANES, cols), BF16),
             pltpu.VMEM((2, count, CHUNK, CHUNK), F32),
             pltpu.VMEM((groups, 8, cols), F32),
-            pltpu.VMEM((1 << levels, 2, groups, STEP, LANES), F32),
-            pltpu.VMEM((2 * levels + 1, 2, groups, STEP, LANES), F32),
+            pltpu.VMEM((1 << levels, 2, width // LANES, LANES), F32),
+            pltpu.VMEM((2 * levels + 1, 2, width // LANES, LANES), F32),
             pltpu.VMEM((groups, depth, cols), BF16),
             pltpu.VMEM((total, width, BLOCK), BF16),
             pltpu.VMEM((groups, 2, rows, cols), BF16),
@@ -499,6 +530,7 @@
             halves,
             pltpu.VMEM((moves, rows, BLOCK), F32),
             pltpu.VMEM((moves, rows, BLOCK), F32),
+            dma((2,)),
             dma((groups,)),
             dma((total,)),
             dma((1 << levels,)),
@@ -516,8 +548,8 @@
             collective_id=0, has_side_effects=True, vmem_limit_bytes=66_000_000
         ),
     )(
-        sequence, state_weight, step_weight, step_bias.reshape(1, heads),
-        decay_rate.reshape(1, heads), skip_gain.reshape(1, heads), input_weight, gate_weight,
+        step_weight.T, step_bias.reshape(1, heads), decay_rate.reshape(1, heads),
+        skip_gain.reshape(1, heads), sequence, state_weight, input_weight, gate_weight,
         output_weight,
     )
 

time: 112 us -> 108 us (0.964)
  Pallas kernels: 107 us -> 105 us
  local copies, waits for them, and re-layouts: 4.17 us -> 2.26 us
    pallas_call x1, Pallas kernels: 107 us -> 105 us  [on_device(): pl.pallas_call(functools.partial(layer_kernel, plan), in_specs=[vmem] * 4...]
    unnamed x2 -> x1, local copies, waits for them, and re-layouts: 4.17 us -> 2.26 us
where the time goes in v2:
time: 108 us
  Pallas kernels  105 us (97%)
  local copies, waits for them, and re-layouts  2.26 us (2%)
    pallas_call x1, Pallas kernels, on_device(): pl.pallas_call(functools.partial(layer_kernel, plan), in_specs=[vmem] * 4...  105 us
    unnamed x1, local copies, waits for them, and re-layouts  2.26 us

profile of v2, /device:TPU:0, one launch (start us, length us, event | category | flops | bytes accessed | tf_op | source)
XLA Modules:
  0.0 107.8 jit_solution(4618712783159536791)
XLA Ops:
  0.0 105.5 %shard_map.91 = bf16[512,1024]{1,0:T(8,128)(2,1)} custom-call(bf16[32,2048]{1,0:T(8,128)(2,1)} %bitcast.4, f32[1,32]{1,0:T(1,128)} %bitcast.5, f32[1,32]{1,0:T(1,128)} %bitcast.6, f32[1,32]{1,0:T(1,128)} %bitcast.7, bf16[512,2048]{1,0:T(8,128)(2,1)} %x_hbm.1, bf16[2048,256]{1,0:T(8,128)(2,1)} %stw_hbm.1, bf16[2048,2048]{1,0:T(8,128)(2,1)} %inw_ref.1, ...), custom_call_target="tpu_custom_call" | custom-call | tf_op jit(solution)/shard_map/pallas_call | solution.py:496
  105.5 2.3 %copy.11 = bf16[512,1024]{1,0:T(8,128)(2,1)} copy(bf16[512,1024]{1,0:T(8,128)(2,1)} %shard_map.91) | data formatting | bytes 2097152
